TPU v7x, 512 devices: a whole 4x8x8 slice. The times are simulated.
512 devices in a mesh: dp: 8 (over z), ctx: 4 (over y_lo, core), tp: 16 (over y_hi, x).
Axes of the slice: x: 4, y: 8 (y_hi: 4, y_lo: 2; y = y_hi * 2 + y_lo), z: 8, core: 2. Of those that a mesh axis runs over, the one named last changes fastest.
Arguments:
- layer_input: bfloat16 [8, 1024, 8192], P('dp', ('ctx', 'tp')), may hold values from -6 to 6
- value_weight: bfloat16 [8192, 4096], P(('dp', 'ctx'), 'tp'), may hold values from -0.0625 to 0.0625
- query_raw: bfloat16 [8, 1024, 4096], P('dp', 'ctx', 'tp'), may hold values from -6 to 6
- key_raw: bfloat16 [8, 1024, 4096], P('dp', 'ctx', 'tp'), may hold values from -6 to 6
- out_grad: bfloat16 [8, 1024, 4096], P('dp', 'ctx', 'tp'), may hold values from -6 to 6
- gate_logits: float32 [2, 8, 32, 1024], P(None, 'dp', 'tp', 'ctx'), may hold values from -14 to 4, as said below
- decay_params: float32 [2, 32], P(None, 'tp'), may hold values from -0.35 to 0.35
- saved_states: float32 [8, 4, 32, 128, 128], P('dp', 'ctx', 'tp'), may hold values from -4 to 4
Outputs:
- input_grad: bfloat16 [8, 1024, 8192], P('dp', ('ctx', 'tp'))
- query_grad: bfloat16 [8, 1024, 4096], P('dp', 'ctx', 'tp')
- key_grad: bfloat16 [8, 1024, 4096], P('dp', 'ctx', 'tp')
- gate_grad: float32 [2, 8, 32, 1024], P(None, 'dp', 'tp', 'ctx')
- decay_grad: float32 [2, 32], P(None, 'tp')
Inputs may be any that keep to these rules, and one draw needn't show every extreme that they name: `gate_logits`: row 0 holds decay logits, row 1 write-strength logits.
All inputs are finite; a program needn't handle non-finite values.
Results may differ from a plain program's by a relative error of at most 0.015.
Values may be sent and summed in bfloat16 or wider, within the bound.
A program may use at most 64 MiB of HBM per device.

v0:
```python
import jax
import jax.numpy as jnp
from jax import lax
from jax.sharding import PartitionSpec as P

SUBLEN = 64


epsilon = 1e-06


def passed_along(shard, axis, by):
    size = lax.axis_size(axis)
    pairs = [(i, i + by) for i in range(size) if 0 <= i + by < size]
    return lax.ppermute(shard, axis, pairs)


def from_everyone(shard, axis):
    copies = jnp.broadcast_to(shard, (lax.axis_size(axis), *shard.shape))
    return lax.all_to_all(copies, axis, split_axis=0, concat_axis=0, tiled=True)


def of_everyone(shard, axis):
    everything = from_everyone(shard, axis)
    return jnp.sum(everything, axis=0)


def inner_step(carried, pieces):
    query_unit, key_unit, values, log_decay, strengths = pieces
    sub_len = query_unit.shape[0]
    head_dim = query_unit.shape[1]
    cumulative = jnp.cumsum(log_decay)
    positions = jnp.arange(sub_len)
    lower_mask = positions[:, None] >= positions[None, :]
    strict_mask = positions[:, None] > positions[None, :]
    spread = jnp.where(lower_mask, cumulative[:, None] - cumulative[None, :], 0.0)
    decays = jnp.where(lower_mask, jnp.exp(spread), 0.0)
    key_gram = jnp.dot(key_unit, key_unit.T)
    system = jnp.eye(sub_len, dtype=jnp.float32) + jnp.where(
        strict_mask, strengths[:, None] * decays * key_gram, 0.0
    )
    right_side = jnp.concatenate(
        [(strengths * jnp.exp(cumulative))[:, None] * key_unit, strengths[:, None] * values], axis=1
    )
    solved = jax.scipy.linalg.solve_triangular(system, right_side, lower=True, unit_diagonal=True)
    new_values = solved[:, head_dim:] - jnp.dot(solved[:, :head_dim], carried)
    scores = decays * jnp.dot(query_unit, key_unit.T)
    output = jnp.dot(query_unit * jnp.exp(cumulative)[:, None], carried) + jnp.dot(
        scores, new_values
    )
    tail_decay = jnp.exp(cumulative[-1] - cumulative)
    updated = jnp.exp(cumulative[-1]) * carried + jnp.dot(
        (key_unit * tail_decay[:, None]).T, new_values
    )
    return (updated, output)


def core(query_row, key_row, values, gate_a, gate_b, params, initial):
    length = query_row.shape[0]
    head_dim = query_row.shape[1]
    query_unit = (
        query_row
        * lax.rsqrt(jnp.sum(query_row * query_row, axis=-1, keepdims=True) + epsilon)
        * head_dim ** (-0.5)
    )
    key_unit = key_row * lax.rsqrt(jnp.sum(key_row * key_row, axis=-1, keepdims=True) + epsilon)
    log_decay = -jnp.exp(params[0]) * jax.nn.softplus(gate_a + params[1])
    strengths = jax.nn.sigmoid(gate_b)
    blocks = length // SUBLEN

    def into_blocks(array):
        return array.reshape((blocks, SUBLEN) + array.shape[1:])

    final_state, outputs = lax.scan(
        inner_step,
        initial,
        (
            into_blocks(query_unit),
            into_blocks(key_unit),
            into_blocks(values),
            into_blocks(log_decay),
            into_blocks(strengths),
        ),
    )
    return (outputs.reshape(length, head_dim), final_state)


def core_heads(query_rows, key_rows, values, gate_a, gate_b, params, initial):
    mapped = jax.vmap(core, in_axes=(0, 0, 0, 0, 0, 1, 0))
    return mapped(query_rows, key_rows, values, gate_a, gate_b, params, initial)


def per_device(
    layer_input, value_weight, query_raw, key_raw, out_grad, gate_logits, decay_params, saved_states
):
    tokens_all = lax.all_gather(layer_input, "tp", axis=1, tiled=True)[0]
    length = tokens_all.shape[0]
    head_dim = saved_states.shape[-1]
    head_count = query_raw.shape[2] // head_dim
    weight_full = lax.all_gather(value_weight, ("dp", "ctx"), axis=0, tiled=True)
    value_flat = jnp.dot(tokens_all, weight_full, preferred_element_type=jnp.float32)
    value_round = value_flat.astype(jnp.bfloat16)

    def split_heads(flat_rows):
        return (
            flat_rows.reshape(length, head_count, head_dim).transpose(1, 0, 2).astype(jnp.float32)
        )

    query_heads = split_heads(query_raw[0])
    key_heads = split_heads(key_raw[0])
    value_heads = split_heads(value_round)
    decay_logit = gate_logits[0, 0]
    strength_logit = gate_logits[1, 0]
    initial_states = saved_states[0, 0]
    outputs, pullback = jax.vjp(
        core_heads,
        query_heads,
        key_heads,
        value_heads,
        decay_logit,
        strength_logit,
        decay_params,
        initial_states,
    )
    cotangent = split_heads(out_grad[0])
    zeros_state = jnp.zeros_like(initial_states)
    incoming = zeros_state
    for section_index in range(lax.axis_size("ctx") - 1):
        leaving = pullback((cotangent, incoming))[6]
        incoming = passed_along(leaving.astype(jnp.bfloat16), "ctx", -1).astype(leaving.dtype)
    gradients = pullback((cotangent, incoming))
    query_grad = (
        gradients[0]
        .transpose(1, 0, 2)
        .reshape(length, head_count * head_dim)
        .astype(jnp.bfloat16)[None]
    )
    key_grad = (
        gradients[1]
        .transpose(1, 0, 2)
        .reshape(length, head_count * head_dim)
        .astype(jnp.bfloat16)[None]
    )
    value_grad = (
        gradients[2].transpose(1, 0, 2).reshape(length, head_count * head_dim).astype(jnp.bfloat16)
    )
    gate_grad = jnp.stack([gradients[3], gradients[4]])[:, None]
    decay_grad = of_everyone(gradients[5], ("dp", "ctx"))
    summed = lax.psum_scatter(
        lax.dot_general(
            value_grad, weight_full, (((1,), (1,)), ((), ())), preferred_element_type=jnp.float32
        ).astype(jnp.bfloat16),
        "tp",
        scatter_dimension=0,
        tiled=True,
    )
    input_grad = summed[None]
    return (input_grad, query_grad, key_grad, gate_grad, decay_grad)


def solution(mesh):
    placed = (
        P("dp", ("ctx", "tp"), None),
        P(("dp", "ctx"), "tp"),
        P("dp", "ctx", "tp"),
        P("dp", "ctx", "tp"),
        P("dp", "ctx", "tp"),
        P(None, "dp", "tp", "ctx"),
        P(None, "tp"),
        P("dp", "ctx", "tp", None, None),
    )
    return jax.shard_map(
        per_device,
        mesh=mesh,
        in_specs=placed,
        out_specs=(
            P("dp", ("ctx", "tp"), None),
            P("dp", "ctx", "tp"),
            P("dp", "ctx", "tp"),
            P(None, "dp", "tp", "ctx"),
            P(None, "tp"),
        ),
        check_vma=False,
    )
```

profile of v0, /device:TPU:1, one launch (start us, length us, event | category | flops | bytes accessed | tf_op | source)
XLA Modules:
  0.0 489.4 jit_solution(7759611729738571562)
XLA Ops:
  13.5 80.4 %all-gather.3.cloned.1.call-done = bf16[1,256,8192]{2,1,0:T(8,128)(2,1)} async-done(((bf16[1,16,8192]{2,1,0:T(8,128)(2,1)}), bf16[1,256,8192]{2,1,0:T(8,128)(2,1)}) %all-gather.3.cloned.1.call-update) | async-done | bytes 4194320 | tf_op jit(solution)/shard_map/all_gather | solution.py:96
  93.9 75.6 %all-gather.5.cloned.1.call-done = bf16[8192,256]{1,0:T(8,128)(2,1)} async-done(((bf16[256,256]{1,0:T(8,128)(2,1)}), bf16[8192,256]{1,0:T(8,128)(2,1)}) %all-gather.5.cloned.1.call-update) | async-done | bytes 4194320 | tf_op jit(solution)/shard_map/all_gather | solution.py:100
  169.5 5.2 %fusion.210 = bf16[256,256]{0,1:T(8,128)(2,1)S(1)} fusion(bf16[8192,256]{1,0:T(8,128)(2,1)} %all-gather.5.cloned.1.call-done, bf16[1,256,8192]{2,1,0:T(8,128)(2,1)} %all-gather.3.cloned.1.call-done), kind=kOutput, calls=%fused_computation.286 | convolution fusion | flops 1073807360 | bytes 8519680 | tf_op jit(solution)/shard_map/dot_general | solution.py:101
  176.6 68.9 %while.135 = (s32[]{:T(128)}, f32[2,128,128]{2,1,0:T(8,128)S(1)}, f32[4,2,64,64]{3,2,1,0:T(8,128)}, bf16[4,2,128,64]{2,3,1,0:T(8,128)(2,1)S(1)}, f32[4,2,64,64]{...) while((s32[]{:T(128)}, f32[2,128,128]{2,1,0:T(8,128)S(1)}, ...), condition=%wide.region_4.5_spmd.clone.clone, body=%wide.region_2.4_spmd.clone.clone.sunk | while | flops 38195776 | bytes 3009961 | solution.py:74
  178.1 9.8 %custom-call.50 = f32[2,1,64,64]{2,3,1,0:T(8,128)S(1)} custom-call(f32[2,1,64,64]{3,2,1,0:T(8,128)S(1)} %add_bitcast_fusion.4), custom_call_target="InvertDiagBlocksLowerTriangular" | custom-call | tf_op jit(solution)/shard_map/jvp(vmap())/while/body/eval_jaxpr/jit(_solve_triangular)/triangular_solve | solution.py:45
  195.4 9.8 %custom-call.50 = f32[2,1,64,64]{2,3,1,0:T(8,128)S(1)} custom-call(f32[2,1,64,64]{3,2,1,0:T(8,128)S(1)} %add_bitcast_fusion.4), custom_call_target="InvertDiagBlocksLowerTriangular" | custom-call | tf_op jit(solution)/shard_map/jvp(vmap())/while/body/eval_jaxpr/jit(_solve_triangular)/triangular_solve | solution.py:45
  212.6 9.8 %custom-call.50 = f32[2,1,64,64]{2,3,1,0:T(8,128)S(1)} custom-call(f32[2,1,64,64]{3,2,1,0:T(8,128)S(1)} %add_bitcast_fusion.4), custom_call_target="InvertDiagBlocksLowerTriangular" | custom-call | tf_op jit(solution)/shard_map/jvp(vmap())/while/body/eval_jaxpr/jit(_solve_triangular)/triangular_solve | solution.py:45
  229.8 9.8 %custom-call.50 = f32[2,1,64,64]{2,3,1,0:T(8,128)S(1)} custom-call(f32[2,1,64,64]{3,2,1,0:T(8,128)S(1)} %add_bitcast_fusion.4), custom_call_target="InvertDiagBlocksLowerTriangular" | custom-call | tf_op jit(solution)/shard_map/jvp(vmap())/while/body/eval_jaxpr/jit(_solve_triangular)/triangular_solve | solution.py:45
  245.5 5.2 %while.137 = (s32[]{:T(128)}, f32[2,128,128]{2,1,0:T(8,128)S(1)}, f32[4,2,1,1]{1,3,2,0:T(1,128)}, bf16[4,2,64,128]{3,2,1,0:T(8,128)(2,1)S(1)}, bf16[4,2,64,128]{...) while((s32[]{:T(128)}, f32[2,128,128]{2,1,0:T(8,128)S(1)}, ...), condition=%wide.region_6.7_spmd.clone, body=%wide.region_5.6_spmd.clone.sunk | while | flops 14893060 | bytes 986779 | solution.py:74
  250.7 2.2 collective-permute-start
  252.9 3.4 collective-permute-done
  256.3 5.2 %while.133 = (s32[]{:T(128)}, f32[2,128,128]{2,1,0:T(8,128)S(1)}, f32[4,2,1,1]{1,3,2,0:T(1,128)}, bf16[4,2,64,128]{3,2,1,0:T(8,128)(2,1)S(1)}, bf16[4,2,64,128]{...) while((s32[]{:T(128)}, f32[2,128,128]{2,1,0:T(8,128)S(1)}, ...), condition=%wide.region_8.9_spmd, body=%wide.region_7.8_spmd.sunk | while | flops 14827523 | bytes 986249 | solution.py:74
  263.4 3.6 collective-permute-done.1
  267.0 5.2 %while.134 = (s32[]{:T(128)}, f32[2,128,128]{2,1,0:T(8,128)S(1)}, f32[4,2,1,1]{1,3,2,0:T(1,128)}, bf16[4,2,64,128]{3,2,1,0:T(8,128)(2,1)S(1)}, bf16[4,2,64,128]{...) while((s32[]{:T(128)}, f32[2,128,128]{2,1,0:T(8,128)S(1)}, ...), condition=%wide.region_10.11_spmd, body=%wide.region_9.10_spmd.sunk | while | flops 14827523 | bytes 986249 | solution.py:74
  274.8 3.0 collective-permute-done.2
  279.9 96.7 %while.136 = (s32[]{:T(128)}, f32[2,128,128]{2,1,0:T(8,128)S(1)}, f32[4,2,64,128]{3,2,0,1:T(8,128)}, f32[4,2,64,128]{3,2,0,1:T(8,128)}, bf16[4,2,64,128]{3,2,0,1...) while((s32[]{:T(128)}, f32[2,128,128]{2,1,0:T(8,128)S(1)}, ...), condition=%wide.region_22.23_spmd.clone.clone, body=%wide.region_11.22_spmd.clone.clone.sunk | while | flops 95114432 | bytes 4842541 | solution.py:74
  283.4 9.8 %custom-call.51 = f32[2,1,64,64]{2,3,1,0:T(8,128)S(1)} custom-call(f32[2,1,64,64]{3,2,1,0:T(8,128)S(1)} %add_bitcast_fusion.5), custom_call_target="InvertDiagBlocksLowerTriangular" | custom-call | tf_op jit(solution)/shard_map/transpose(jvp(vmap()))/while/body/eval_jaxpr/jit(_solve_triangular)/triangular_solve | solution.py:45
  307.5 9.8 %custom-call.51 = f32[2,1,64,64]{2,3,1,0:T(8,128)S(1)} custom-call(f32[2,1,64,64]{3,2,1,0:T(8,128)S(1)} %add_bitcast_fusion.5), custom_call_target="InvertDiagBlocksLowerTriangular" | custom-call | tf_op jit(solution)/shard_map/transpose(jvp(vmap()))/while/body/eval_jaxpr/jit(_solve_triangular)/triangular_solve | solution.py:45
  331.8 9.8 %custom-call.51 = f32[2,1,64,64]{2,3,1,0:T(8,128)S(1)} custom-call(f32[2,1,64,64]{3,2,1,0:T(8,128)S(1)} %add_bitcast_fusion.5), custom_call_target="InvertDiagBlocksLowerTriangular" | custom-call | tf_op jit(solution)/shard_map/transpose(jvp(vmap()))/while/body/eval_jaxpr/jit(_solve_triangular)/triangular_solve | solution.py:45
  355.9 9.8 %custom-call.51 = f32[2,1,64,64]{2,3,1,0:T(8,128)S(1)} custom-call(f32[2,1,64,64]{3,2,1,0:T(8,128)S(1)} %add_bitcast_fusion.5), custom_call_target="InvertDiagBlocksLowerTriangular" | custom-call | tf_op jit(solution)/shard_map/transpose(jvp(vmap()))/while/body/eval_jaxpr/jit(_solve_triangular)/triangular_solve | solution.py:45
  377.6 5.5 %convolution_convert_fusion = bf16[256,8192]{1,0:T(8,128)(2,1)} fusion(bf16[256,256]{0,1:T(8,128)(2,1)S(1)} %bitcast.659, bf16[8192,256]{1,0:T(8,128)(2,1)} %all-gather.5.cloned.1.call-done), kind=kOutput, calls=%fused_computation.283 | convolution fusion | flops 1075838976 | bytes 8519680 | tf_op jit(solution)/shard_map/dot_general | solution.py:150
  384.6 5.9 %all-to-all-start = ((f32[32,2,2]{2,1,0:T(2,128)}), f32[32,2,2]{2,1,0:T(2,128)S(1)}, u32[]{:S(2)}, u32[]{:S(2)}) async-start(f32[32,2,2]{2,1,0:T(2,128)} %broadcast_in_dim.279), calls=%async_computation.1 | async-start | bytes 65536 | tf_op jit(solution)/shard_map/all_to_all | solution.py:20
  393.6 5.1 %all-to-all-done = f32[32,2,2]{2,1,0:T(2,128)S(1)} async-done(((f32[32,2,2]{2,1,0:T(2,128)}), f32[32,2,2]{2,1,0:T(2,128)S(1)}, u32[]{:S(2)}, u32[]{:S(2)}) %all-to-all-start) | async-done | bytes 544 | tf_op jit(solution)/shard_map/all_to_all | solution.py:20
  399.3 83.6 %reduce-scatter.2.cloned.1.call-done = bf16[16,8192]{1,0:T(8,128)(2,1)} async-done(((bf16[256,8192]{1,0:T(8,128)(2,1)}), bf16[16,8192]{1,0:T(8,128)(2,1)}) %reduce-scatter.2.cloned.1.call-update) | async-done | bytes 262160 | tf_op jit(solution)/shard_map/reduce_scatter | solution.py:149
  (428 shorter events, 121.8 us)
Async XLA Ops:
  7.2 5.2 %copy-start.3 = (bf16[1,256,256]{2,1,0:T(8,128)(2,1)S(1)}, bf16[1,256,256]{2,1,0:T(8,128)(2,1)}, u32[]{:S(2)}) copy-start(bf16[1,256,256]{2,1,0:T(8,128)(2,1)} %param.22) | copy-start | bytes 393220
  7.2 5.6 %copy-start.19 = (f32[2,2]{1,0:T(2,128)S(1)}, f32[2,2]{1,0:T(2,128)}, u32[]{:S(2)}) copy-start(f32[2,2]{1,0:T(2,128)} %param.24) | copy-start | bytes 52
  7.2 86.7 %all-gather.3.cloned.1.call-start = ((), (), s32[]{:S(2)}) async-start(), calls=%async_computation.2 | async-start | bytes 4456448 | tf_op jit(solution)/shard_map/all_gather | solution.py:96
  7.9 161.6 %all-gather.5.cloned.1.call-start = ((), (), s32[]{:S(2)}) async-start(), calls=%async_computation.3 | async-start | bytes 4325376 | tf_op jit(solution)/shard_map/all_gather | solution.py:100
  8.7 474.2 %reduce-scatter.2.cloned.1.call-start = ((), (), s32[]{:S(2)}) async-start(), calls=%async_computation.4 | async-start | bytes 4456448 | tf_op jit(solution)/shard_map/reduce_scatter | solution.py:149
  9.6 2.5 copy-start.10
  10.9 1.8 copy-start.6
  10.9 1.7 copy-start.4
  12.8 161.9 %copy-start.15 = (f32[2]{0:T(128)}, f32[2]{0:T(128)S(1)}, u32[]{:S(2)}) copy-start(f32[2]{0:T(128)S(1)} %get-tuple-element.2979) | copy-start | bytes 28
  12.8 161.9 %copy-start.17 = (f32[2]{0:T(128)}, f32[2]{0:T(128)S(1)}, u32[]{:S(2)}) copy-start(f32[2]{0:T(128)S(1)} %get-tuple-element.2980) | copy-start | bytes 28
  13.5 163.0 %copy-start = (f32[1,1,2,128,128]{4,3,2,1,0:T(8,128)S(1)}, f32[1,1,2,128,128]{4,3,2,1,0:T(8,128)}, u32[]{:S(2)}) copy-start(f32[1,1,2,128,128]{4,3,2,1,0:T(8,128)} %param.25) | copy-start | bytes 393220
  250.7 5.6 %collective-permute-start = (bf16[2,128,128]{2,1,0:T(8,128)(2,1)S(1)}, bf16[2,128,128]{2,1,0:T(8,128)(2,1)S(1)}, u32[]{:S(2)}, u32[]{:S(2)}) collective-permute-start(bf16[2,128,128]{2,1,0:T(8,128)(2,1)S(1)} %convert_element_type.125), channel_id=1, source_target_pairs={{16,0},{32,16},{48,32},{17,1},{33,17},{49,33},{18,2},{34,18},{50,3... | collective-permute-start | bytes 196616 | tf_op jit(solution)/shard_map/ppermute | solution.py:15
  261.4 5.6 %collective-permute-start.1 = (bf16[2,128,128]{2,1,0:T(8,128)(2,1)S(1)}, bf16[2,128,128]{2,1,0:T(8,128)(2,1)S(1)}, u32[]{:S(2)}, u32[]{:S(2)}) collective-permute-start(bf16[2,128,128]{2,1,0:T(8,128)(2,1)S(1)} %convert_element_type.127), channel_id=1, source_target_pairs={{16,0},{32,16},{48,32},{17,1},{33,17},{49,33},{18,2},{34,18},{50,3... | collective-permute-start | bytes 196616 | tf_op jit(solution)/shard_map/ppermute | solution.py:15
  272.2 5.6 %collective-permute-start.2 = (bf16[2,128,128]{2,1,0:T(8,128)(2,1)S(1)}, bf16[2,128,128]{2,1,0:T(8,128)(2,1)S(1)}, u32[]{:S(2)}, u32[]{:S(2)}) collective-permute-start(bf16[2,128,128]{2,1,0:T(8,128)(2,1)S(1)} %convert_element_type.129), channel_id=1, source_target_pairs={{16,0},{32,16},{48,32},{17,1},{33,17},{49,33},{18,2},{34,18},{50,3... | collective-permute-start | bytes 196616 | tf_op jit(solution)/shard_map/ppermute | solution.py:15
  383.1 0.9 copy-start.20
  383.1 7.5 %copy-start.13 = (f32[4,2,64]{2,1,0:T(2,128)S(1)}, f32[4,2,64]{2,1,0:T(2,128)}, u32[]{:S(2)}) copy-start(f32[4,2,64]{2,1,0:T(2,128)} %get-tuple-element.1874) | copy-start | bytes 6148
  383.1 7.7 %copy-start.2 = (f32[4,2,64,128]{3,2,0,1:T(8,128)S(1)}, f32[4,2,64,128]{3,2,0,1:T(8,128)}, u32[]{:S(2)}) copy-start(f32[4,2,64,128]{3,2,0,1:T(8,128)} %get-tuple-element.1872) | copy-start | bytes 786436
  383.1 7.8 %copy-start.1 = (f32[4,2,64,128]{3,2,0,1:T(8,128)S(1)}, f32[4,2,64,128]{3,2,0,1:T(8,128)}, u32[]{:S(2)}) copy-start(f32[4,2,64,128]{3,2,0,1:T(8,128)} %get-tuple-element.1871) | copy-start | bytes 786436
  383.1 8.0 %copy-start.11 = (f32[1,1,2,256]{3,2,1,0:T(2,128)S(1)}, f32[1,1,2,256]{3,2,1,0:T(2,128)}, u32[]{:S(2)}) copy-start(f32[1,1,2,256]{3,2,1,0:T(2,128)} %copy-done.10) | copy-start | bytes 6148
  383.1 8.0 %copy-start.7 = (f32[2,256]{1,0:T(2,128)S(1)}, f32[2,256]{1,0:T(2,128)}, u32[]{:S(2)}) copy-start(f32[2,256]{1,0:T(2,128)} %copy-done.6) | copy-start | bytes 6148
  383.1 8.1 %copy-start.14 = (f32[2,1,2,256]{3,2,1,0:T(2,128)S(1)}, f32[2,1,2,256]{3,2,1,0:T(2,128)}, u32[]{:S(2)}) copy-start(f32[2,1,2,256]{3,2,1,0:T(2,128)} %param.23) | copy-start | bytes 12292
  383.2 8.1 %copy-start.9 = (f32[2,256]{1,0:T(2,128)S(1)}, f32[2,256]{1,0:T(2,128)}, u32[]{:S(2)}) copy-start(f32[2,256]{1,0:T(2,128)} %copy-done.8) | copy-start | bytes 6148
  383.2 8.2 %copy-start.5 = (f32[2,256]{1,0:T(2,128)S(1)}, f32[2,256]{1,0:T(2,128)}, u32[]{:S(2)}) copy-start(f32[2,256]{1,0:T(2,128)} %copy-done.4) | copy-start | bytes 6148
  384.6 14.1 %all-to-all-start = ((f32[32,2,2]{2,1,0:T(2,128)}), f32[32,2,2]{2,1,0:T(2,128)S(1)}, u32[]{:S(2)}, u32[]{:S(2)}) async-start(f32[32,2,2]{2,1,0:T(2,128)} %broadcast_in_dim.279), calls=%async_computation.1 | async-start | bytes 65536 | tf_op jit(solution)/shard_map/all_to_all | solution.py:20
  (4 other events, 2.6 us)
Sparse Core Ops, SparseCore 0:
  11.0 82.8 all-gather.2
  96.1 73.4 all-gather.4
  383.3 99.5 reduce-scatter.1
where the time goes:
time: 492 us; the launch traced here: 489 us
  waiting for transfers between devices  256 us (52%)
  other arithmetic  102 us (21%)
  matrix products  63.2 us (13%)
  local copies, waits for them, and re-layouts  40.8 us (8%)
  between operations  14.5 us (3%)
  starting transfers between devices  12.1 us (2%)
    reduce_scatter x1, waiting for transfers between devices, per_device(): lax.psum_scatter(lax.dot_general(value_grad, weight_full, (((1,), (1,)),...  83.6 us
    another operation x36, other arithmetic, inner_step(): jax.scipy.linalg.solve_triangular(system, right_side, lower=True, unit_di...  83.2 us
    all_gather x1, waiting for transfers between devices, per_device(): tokens_all = lax.all_gather(layer_input, 'tp', axis=1, tiled=True)[0]  80.4 us
    all_gather x1, waiting for transfers between devices, per_device(): lax.all_gather(value_weight, ('dp', 'ctx'), axis=0, tiled=True)  75.6 us
    mul x16, local copies, waits for them, and re-layouts, inner_step(): jnp.exp(cumulative[-1]) * carried  10.1 us
    ppermute x3, waiting for transfers between devices, passed_along(): return lax.ppermute(shard, axis, pairs)  9.94 us
    another operation x12, matrix products, inner_step(): jax.scipy.linalg.solve_triangular(system, right_side, lower=True, unit_di...  9.86 us
  transfers between devices with their start and end apart: 7, of which 7 were waited for; matrix products, arithmetic and copies ran while one was open for 2% of the time, Pallas kernels for 0%

commit v1 on v0

v1 whole, which is shorter than its diff:
```python
import jax
import jax.numpy as jnp
from jax import lax
from jax.experimental import pallas as pl
from jax.experimental.pallas import tpu as pltpu
from jax.sharding import PartitionSpec as P

f32 = jnp.float32
bf16 = jnp.bfloat16
EPS = 1e-6
MESH = pl.DeviceIdType.MESH

ZN, YN, XN = 8, 8, 4
N, HD, HEADS = 256, 128, 2
TOK = 16
KB = 1024
D = 8192


def mm(a, b, ca=1, cb=0):
    return lax.dot_general(
        a.astype(bf16), b.astype(bf16), (((ca,), (cb,)), ((), ())), preferred_element_type=f32
    )


def exact(a, b):
    return lax.dot_general(
        a, b, (((1,), (0,)), ((), ())), preferred_element_type=f32, precision=lax.Precision.HIGHEST
    )


def softplus(x):
    u = jnp.exp(-jnp.abs(x))
    w = 1.0 + u
    tail = jnp.where(w == 1.0, u, jnp.log(w) * u / jnp.where(w == 1.0, 1.0, w - 1.0))
    return jnp.maximum(x, 0.0) + tail


def sigmoid(x):
    return 1.0 / (1.0 + jnp.exp(-x))


def pair(shape, dim, first, second):
    return jnp.where(lax.broadcasted_iota(jnp.int32, shape, dim) == 0, first, second)


def kernel(
    x_ref, w_ref, q_ref, k_ref, do_ref, gl_ref, par_ref, st_ref,
    ig_ref, qg_ref, kg_ref, gg_ref, dg_ref,
    xs, xg, xl, wg, pcs, pcr, cbs, cbr, dvs, dvg, vp, vr, gl_s, gs, gx, gys, gyr, dct, dzt,
    qn, kn, dec, a_s, p_s, t_s, ef_s, dr_s, s_in,
    xa_s, xa_r, xx_s, xx_r, wp_s, wp_r, wz_s, wz_r, wd_s, wd_r, pc_s, pc_r, cb_s, cb_r,
    dv_s, dv_r, vp_s, vp_r, gx_s, gx_r, gy_s, gy_r, dc_s, dc_r, dz_s, dz_r,
):
    z = lax.axis_index("dp")
    ctx = lax.axis_index("ctx")
    tp = lax.axis_index("tp")
    ylo, c = lax.div(ctx, 2), lax.rem(ctx, 2)
    yhi, x = lax.div(tp, XN), lax.rem(tp, XN)
    yy = yhi * 2 + ylo

    def at(z_, yy_, c_, x_):
        return {
            "dp": z_,
            "ctx": lax.rem(yy_, 2) * 2 + c_,
            "tp": lax.div(yy_, 2) * XN + x_,
        }

    def y_at(o):
        return lax.rem(yy + o, YN)

    def z_at(o):
        return lax.rem(z + o, ZN)

    def x_at(o):
        return lax.rem(x + o, XN)

    def send(src, dst, s, r, device):
        return pltpu.make_async_remote_copy(
            src_ref=src, dst_ref=dst, send_sem=s, recv_sem=r, device_id=device, device_id_type=MESH
        )

    barrier = pltpu.get_barrier_semaphore()
    peers = [at(z, y_at(o), c, x) for o in range(1, YN)]
    peers += [at(z, y_at(o), 1 - c, x) for o in range(YN)]
    peers += [at(z, yy, c, x_at(o)) for o in range(1, XN)]
    peers += [at(z_at(o), yy, c, x) for o in range(1, ZN)]
    for peer in peers:
        pl.semaphore_signal(barrier, inc=1, device_id=peer, device_id_type=MESH)

    for y_ in range(YN):
        for z_ in range(ZN):
            xs[y_, :, z_ * 128 : (z_ + 1) * 128] = x_ref[
                :, z_ * KB + y_ * 128 : z_ * KB + (y_ + 1) * 128
            ]
    xg[x, yy] = xs[yy]
    pl.semaphore_wait(barrier, len(peers))

    to_core = lax.rem(lax.div(yhi, 2) + 1 + lax.div(ctx, 2) + lax.rem(ctx, 2), 2)
    own_half = lax.rem(c + 1 + lax.div(yhi, 2) + lax.rem(yhi, 2), 2)
    w_pre = [
        send(
            w_ref.at[pl.ds(h * 128, 128), :],
            wg.at[lax.div(yhi, 2), z, lax.rem(yhi, 2)],
            wp_s.at[h],
            wp_r.at[lax.rem(yhi, 2)],
            at(z, ctx * 2 + h, to_core, x),
        )
        for h in range(2)
    ]
    w_pre_in = [
        send(w_ref.at[pl.ds(0, 128), :], wg.at[own_half, z, h], wp_s.at[h], wp_r.at[h], at(z, yy, 1 - c, x))
        for h in range(2)
    ]
    for copy in w_pre:
        copy.start()
    x_all = [
        send(xs.at[y_at(o)], xg.at[x, yy], xa_s.at[o], xa_r.at[o], at(z, y_at(o), c, x))
        for o in range(1, YN)
    ]
    for copy in x_all:
        copy.start()

    def w_round():
        for copy in w_pre_in:
            copy.wait_recv()
        for copy in w_sends:
            copy.start()

    w_sends = [
        send(wg.at[own_half, z], wg.at[own_half, z], wz_s.at[o], wz_r.at[o], at(z_at(o), yy, c, x))
        for o in range(1, ZN)
    ]
    x_sends = [
        send(xg.at[x], xg.at[x], xx_s.at[o], xx_r.at[o], at(z, yy, c, x_at(o)))
        for o in range(1, XN)
    ]

    def x_round():
        for copy in x_all:
            copy.wait_recv()
        for copy in x_sends:
            copy.start()

    ii = lax.broadcasted_iota(jnp.int32, (N, N), 0)
    jj = lax.broadcasted_iota(jnp.int32, (N, N), 1)
    low = ii >= jj
    strict = ii > jj
    apart = ii ^ jj
    p0 = pair((HEADS, 1), 0, par_ref[0, 0], par_ref[0, 1])
    p1 = pair((HEADS, 1), 0, par_ref[1, 0], par_ref[1, 1])
    ga = gl_ref[0, 0]
    ld = -jnp.exp(p0) * softplus(ga + p1)
    be = sigmoid(gl_ref[1, 0])
    pad4 = jnp.zeros((4, N), f32)
    upto = jnp.where(ii <= jj, 1.0, 0.0)
    g_rows = exact(jnp.concatenate([ld, be, pad4], axis=0), upto)
    rows = jnp.concatenate([g_rows[:HEADS], be, pad4, jnp.zeros((120, N), f32)], axis=0)
    columns = rows.T
    g_col = [columns[:, h : h + 1] for h in range(HEADS)]
    be_col = [columns[:, HEADS + h : HEADS + h + 1] for h in range(HEADS)]
    gam = [jnp.exp(g) for g in g_col]
    tau = [jnp.exp(g[N - 1 : N, :] - g) for g in g_col]
    gam_n = [jnp.exp(g[N - 1 : N, :]) for g in g_col]

    def head(ref, h):
        return ref[:, h * HD : (h + 1) * HD]

    def inverse_norm(raw):
        return lax.rsqrt(jnp.sum(raw * raw, axis=-1, keepdims=True) + EPS)

    for h in range(HEADS):
        q_raw = head(q_ref, h).astype(f32)
        k_raw = head(k_ref, h).astype(f32)
        qn[h] = q_raw * (inverse_norm(q_raw) * HD**-0.5)
        kn[h] = k_raw * inverse_norm(k_raw)
        dec[h] = jnp.where(low, jnp.exp(jnp.where(low, g_col[h] - g_rows[h : h + 1], 0.0)), 0.0)
        a_s[h] = jnp.where(strict, be_col[h] * dec[h] * mm(kn[h], kn[h], 1, 1), 0.0)
        p_s[h] = dec[h] * mm(qn[h], kn[h], 1, 1)
        t_s[h] = jnp.where(ii == jj, 1.0, jnp.where(apart == 1, -a_s[h], 0.0))
    w_round()

    size = 2
    while size < N:
        for h in range(HEADS):
            level = jnp.where((apart >= size) & (apart < 2 * size), a_s[h], 0.0)
            t_b = t_s[h].astype(bf16)
            t_s[h] = t_s[h] - mm(mm(t_b, level), t_b)
        size *= 2
    x_round()

    for h in range(HEADS):
        do_h = head(do_ref, h)
        start = mm(p_s[h], do_h, 0, 0)
        ef_s[h] = mm(t_s[h], jnp.concatenate([start, kn[h] * tau[h]], axis=1), 0, 0)
        ke = mm(kn[h] * (be_col[h] * gam[h]), ef_s[h], 0, 0)
        const = mm(qn[h] * gam[h], do_h, 0, 0) - ke[:, :HD]
        i2 = lax.broadcasted_iota(jnp.int32, (HD, HD), 0)
        j2 = lax.broadcasted_iota(jnp.int32, (HD, HD), 1)
        carry = jnp.where(i2 == j2, gam_n[h], 0.0) - ke[:, HD:]
        pcs[h] = jnp.concatenate([carry, const], axis=1).astype(bf16)

    to_partner = send(pcs, pcr, pc_s, pc_r, at(z, yy, 1 - c, x))
    to_partner.start()
    to_partner.wait_recv()
    other_y = yy + 1 - 2 * ylo
    even = c == 0
    for h in range(HEADS):
        mine, theirs = pcs[h], pcr[h]
        first = jnp.where(even, mine, theirs)
        last = jnp.where(even, theirs, mine)
        cbs[h] = (mm(first[:, :HD], last[:, HD:]) + first[:, HD:].astype(f32)).astype(bf16)
    to_other = send(cbs, cbr, cb_s, cb_r, at(z, other_y, c, x))
    to_other.start()
    to_other.wait_recv()
    for h in range(HEADS):
        inward = jnp.where(ylo == 0, cbr[h], jnp.zeros((HD, HD), bf16))
        theirs = pcr[h]
        through = mm(theirs[:, :HD], inward) + theirs[:, HD:].astype(f32)
        s_in[h] = jnp.where(even, through, inward.astype(f32))
        dr = ef_s[h][:, :HD] + mm(ef_s[h][:, HD:], s_in[h])
        dr_s[h] = dr
        dvs[:, h * HD : (h + 1) * HD] = (be_col[h] * dr).astype(bf16)
    dv_sends = [
        send(dvs, dvg.at[yy], dv_s.at[o], dv_r.at[o], at(z, y_at(o), c, x)) for o in range(1, YN)
    ]
    for copy in dv_sends:
        copy.start()
    dvg[yy] = dvs[...]

    for copy in w_sends:
        copy.wait_recv()
    w_share = send(wg.at[own_half], wg.at[own_half], wd_s, wd_r, at(z, yy, 1 - c, x))
    w_share.start()
    for copy in x_sends:
        copy.wait_recv()
    for x_ in range(XN):
        for y_ in range(YN):
            row = (y_ % 2) * N + ((y_ // 2) * XN + x_) * TOK
            xl[row : row + TOK, :] = xg[x_, y_]
    w_share.wait_recv()

    def weight(y_hi):
        return wg[lax.div(y_hi, 2), :, lax.rem(y_hi, 2)].reshape(KB, N)

    def v_piece(o, _):
        d = lax.rem(yy + o, YN)
        rows_in = xl[pl.ds(pl.multiple_of(lax.rem(d, 2) * N, N), N), :]
        vp[d] = mm(rows_in, weight(lax.div(d, 2))).astype(bf16)
        return 0

    def v_send(o):
        return send(vp.at[y_at(o)], vr.at[yy], vp_s.at[o], vp_r.at[o], at(z, y_at(o), c, x))

    def v_step(o, _):
        v_piece(o, 0)
        v_send(o).start()
        return 0

    lax.fori_loop(1, YN, v_step, 0)
    v_piece(0, 0)
    vr[yy] = vp[yy]

    for copy in dv_sends:
        copy.wait_recv()

    def g_piece(o):
        x_to = x_at(o)
        for y_ in range(YN):
            row = pl.multiple_of((y_ // 2) * (XN * TOK) + x_to * TOK, TOK)
            for h in range(YN // 2):
                gl_s[y_ * TOK : (y_ + 1) * TOK, h * N : (h + 1) * N] = dvg[
                    h * 2 + y_ % 2, pl.ds(row, TOK), :
                ]
        total = jnp.zeros((YN * TOK, KB), f32)
        for h in range(YN // 2):
            total = total + mm(gl_s[:, h * N : (h + 1) * N], weight(h), 1, 1)
        gs[x_to] = total.astype(bf16)

    def g_send(o):
        return send(gs.at[x_at(o)], gx.at[x], gx_s.at[o], gx_r.at[o], at(z, yy, c, x_at(o)))

    def g_step(o, _):
        g_piece(o)
        g_send(o).start()
        return 0

    lax.fori_loop(1, XN, g_step, 0)
    g_piece(0)
    for o in range(1, XN):
        g_send(o).wait_recv()
    gx[x] = gs[x]
    gys[...] = (
        (gx[0].astype(f32) + gx[1].astype(f32)) + (gx[2].astype(f32) + gx[3].astype(f32))
    ).astype(bf16)
    gy_sends = [
        send(
            gys.at[pl.ds(pl.multiple_of(y_at(o) * TOK, TOK), TOK), :],
            gyr.at[yy], gy_s.at[o], gy_r.at[o], at(z, y_at(o), c, x),
        )
        for o in range(1, YN)
    ]
    for copy in gy_sends:
        copy.start()
    gyr[yy] = gys[pl.ds(pl.multiple_of(yy * TOK, TOK), TOK), :]

    for o in range(1, YN):
        v_send(o).wait_recv()
    values = vr[0].astype(f32)
    for y_ in range(1, YN):
        values = values + vr[y_].astype(f32)
    dvs2 = values.astype(bf16)
    lane = lax.broadcasted_iota(jnp.int32, (N, HD), 1)
    picked = jnp.zeros((N, HD), f32)
    dg_rows = []
    for h in range(HEADS):
        state = st_ref[0, 0, h]
        q_u, k_u = qn[h], kn[h]
        q_b, k_b = q_u.astype(bf16), k_u.astype(bf16)
        d_state, dr = s_in[h], dr_s[h]
        base = dvs2[:, h * HD : (h + 1) * HD].astype(f32) - gam[h] * mm(k_b, state)
        new = mm(t_s[h], be_col[h] * base).astype(bf16)
        do_h = head(do_ref, h)
        both = jnp.concatenate([do_h, dr.astype(bf16)], axis=0)
        cross = mm(both, new, 1, 1)
        by_state = mm(both, state, 1, 1)
        d_p = cross[:N]
        d_a = jnp.where(strict, -cross[N:], 0.0)
        scores = (d_p * dec[h]).astype(bf16)
        gram = (d_a * dec[h] * be_col[h]).astype(bf16)
        da_a = d_a * a_s[h]
        mass = d_p * p_s[h] + da_a
        o_part = gam[h] * by_state[:N]
        r_part = (be_col[h] * gam[h]) * by_state[N:]
        t_part = tau[h] * mm(new, d_state, 1, 1)
        d_q = mm(scores, k_b) + o_part
        d_k = mm(scores, q_b, 0, 0) + mm(gram, k_b) + mm(gram, k_b, 0, 0) - r_part + t_part
        d_be = be_col[h] * jnp.sum(dr * base, axis=1, keepdims=True) + jnp.sum(
            da_a, axis=1, keepdims=True
        )
        tail = jnp.sum(t_part * k_u, axis=1, keepdims=True)
        dg_c = (
            jnp.sum(mass, axis=1, keepdims=True)
            + jnp.sum(o_part * q_u - r_part * k_u, axis=1, keepdims=True)
            - tail
        )
        dg_n = jnp.sum(tail, axis=0, keepdims=True) + gam_n[h] * jnp.sum(
            jnp.sum(state * d_state, axis=1, keepdims=True), axis=0, keepdims=True
        )
        last = lax.broadcasted_iota(jnp.int32, (1, N), 1) == N - 1
        dg_rows.append(jnp.where(last, dg_n, 0.0) - jnp.sum(mass, axis=0, keepdims=True))
        picked = jnp.where(lane == h, dg_c, jnp.where(lane == HEADS + h, d_be, picked))

        def through_norm(d_unit, raw_ref, scale):
            raw = head(raw_ref, h).astype(f32)
            inverse = inverse_norm(raw)
            unit = raw * inverse
            inner = jnp.sum(unit * d_unit, axis=1, keepdims=True)
            return (scale * inverse) * (d_unit - unit * inner)

        qg_ref[0, :, h * HD : (h + 1) * HD] = through_norm(d_q, q_ref, HD**-0.5).astype(bf16)
        kg_ref[0, :, h * HD : (h + 1) * HD] = through_norm(d_k, k_ref, 1.0).astype(bf16)

    picked_rows = picked.T
    dg = picked_rows[:HEADS] + jnp.concatenate(dg_rows, axis=0)
    onward = jnp.where(low, 1.0, 0.0)
    d_ld = exact(jnp.concatenate([dg, jnp.zeros((6, N), f32)], axis=0), onward)[:HEADS]
    d_ga = d_ld * (-jnp.exp(p0)) * sigmoid(ga + p1)
    gg_ref[0, 0] = d_ga
    gg_ref[1, 0] = picked_rows[HEADS : 2 * HEADS] * (1.0 - be)
    scale_sum = jnp.sum(d_ld * ld, axis=1, keepdims=True)
    bias_sum = jnp.sum(d_ga, axis=1, keepdims=True)
    lane2 = lax.broadcasted_iota(jnp.int32, (HEADS, 128), 1)
    mine = jnp.where(lane2 == 0, scale_sum, jnp.where(lane2 == 1, bias_sum, 0.0))
    dct[ctx] = jnp.concatenate([mine, jnp.zeros((6, 128), f32)], axis=0)
    dc_sends = []
    for o, (dy, dc) in enumerate(((0, 1), (1, 0), (1, 1))):
        y_to = yy + dy * (1 - 2 * ylo)
        c_to = c + dc * (1 - 2 * c)
        dc_sends.append(send(dct.at[ctx], dct.at[ctx], dc_s.at[o], dc_r.at[o], at(z, y_to, c_to, x)))
    for copy in dc_sends:
        copy.start()
    for copy in dc_sends:
        copy.wait_recv()
    dzt[z] = (dct[0] + dct[1]) + (dct[2] + dct[3])
    dz_sends = [
        send(dzt.at[z], dzt.at[z], dz_s.at[o], dz_r.at[o], at(z_at(o), yy, c, x))
        for o in range(1, ZN)
    ]
    for copy in dz_sends:
        copy.start()

    for copy in gy_sends:
        copy.wait_recv()
    for y_ in range(YN):
        for z_ in range(ZN):
            ig_ref[0, :, z_ * KB + y_ * 128 : z_ * KB + (y_ + 1) * 128] = gyr[
                y_, :, z_ * 128 : (z_ + 1) * 128
            ]
    for copy in dz_sends:
        copy.wait_recv()
    grand = dzt[0]
    for z_ in range(1, ZN):
        grand = grand + dzt[z_]
    dg_ref[...] = pair(
        (2, 2), 0,
        pair((2, 2), 1, grand[0:1, 0:1], grand[1:2, 0:1]),
        pair((2, 2), 1, grand[0:1, 1:2], grand[1:2, 1:2]),
    )

    for copy in w_pre + x_all + w_sends + x_sends:
        copy.wait_send()
    for copy in [to_partner, to_other, w_share] + dv_sends:
        copy.wait_send()
    for o in range(1, YN):
        v_send(o).wait_send()
    for o in range(1, XN):
        g_send(o).wait_send()
    for copy in gy_sends + dc_sends + dz_sends:
        copy.wait_send()


def per_device(
    layer_input, value_weight, query_raw, key_raw, out_grad, gate_logits, decay_params, saved_states
):
    vmem = pl.BlockSpec(memory_space=pltpu.VMEM)
    dma = pltpu.SemaphoreType.DMA
    V = pltpu.VMEM
    counts = (8, 8, 4, 4, 2, 2, 8, 8, None, None, None, None, None, None)
    counts += (8, 8, 8, 8, 4, 4, 8, 8, 3, 3, 8, 8)
    return pl.pallas_call(
        kernel,
        out_shape=(
            jax.ShapeDtypeStruct((1, TOK, D), bf16),
            jax.ShapeDtypeStruct((1, N, N), bf16),
            jax.ShapeDtypeStruct((1, N, N), bf16),
            jax.ShapeDtypeStruct((2, 1, HEADS, N), f32),
            jax.ShapeDtypeStruct((2, HEADS), f32),
        ),
        in_specs=[vmem] * 6 + [pl.BlockSpec(memory_space=pltpu.SMEM), vmem],
        out_specs=(vmem,) * 5,
        scratch_shapes=[
            V((YN, TOK, KB), bf16),
            V((XN, YN, TOK, KB), bf16),
            V((2 * N, KB), bf16),
            V((2, ZN, 2, 128, N), bf16),
            V((HEADS, HD, 2 * HD), bf16),
            V((HEADS, HD, 2 * HD), bf16),
            V((HEADS, HD, HD), bf16),
            V((HEADS, HD, HD), bf16),
            V((N, N), bf16),
            V((YN, N, N), bf16),
            V((YN, N, N), bf16),
            V((YN, N, N), bf16),
            V((YN * TOK, KB), bf16),
            V((XN, YN * TOK, KB), bf16),
            V((XN, YN * TOK, KB), bf16),
            V((YN * TOK, KB), bf16),
            V((YN, TOK, KB), bf16),
            V((4, 8, 128), f32),
            V((ZN, 8, 128), f32),
            V((HEADS, N, HD), f32),
            V((HEADS, N, HD), f32),
            V((HEADS, N, N), f32),
            V((HEADS, N, N), f32),
            V((HEADS, N, N), f32),
            V((HEADS, N, N), f32),
            V((HEADS, N, 2 * HD), f32),
            V((HEADS, N, HD), f32),
            V((HEADS, HD, HD), f32),
        ]
        + [dma(()) if n is None else dma((n,)) for n in counts],
        compiler_params=pltpu.CompilerParams(
            collective_id=0, has_side_effects=True, vmem_limit_bytes=56 * 2**20
        ),
    )(
        layer_input[0], value_weight, query_raw[0], key_raw[0], out_grad[0],
        gate_logits, decay_params, saved_states,
    )


def solution(mesh):
    placed = (
        P("dp", ("ctx", "tp"), None),
        P(("dp", "ctx"), "tp"),
        P("dp", "ctx", "tp"),
        P("dp", "ctx", "tp"),
        P("dp", "ctx", "tp"),
        P(None, "dp", "tp", "ctx"),
        P(None, "tp"),
        P("dp", "ctx", "tp", None, None),
    )
    return jax.shard_map(
        per_device,
        mesh=mesh,
        in_specs=placed,
        out_specs=(
            P("dp", ("ctx", "tp"), None),
            P("dp", "ctx", "tp"),
            P("dp", "ctx", "tp"),
            P(None, "dp", "tp", "ctx"),
            P(None, "tp"),
        ),
        check_vma=False,
    )
```

time: 492 us -> 101 us (0.21)
  waiting for transfers between devices: 256 us -> 0 us
  other arithmetic: 102 us -> 0 us
  Pallas kernels: 0 us -> 94.4 us
  matrix products: 63.2 us -> 0 us
  local copies, waits for them, and re-layouts: 40.8 us -> 4.55 us
  between operations: 14.5 us -> 0.66 us
  starting transfers between devices: 12.1 us -> 0 us
    all_gather x2 -> x0, waiting for transfers between devices: 156 us -> none  [the longest x1 80.4 us: per_device(): tokens_all = lax.all_gather(layer_input, 'tp', axis=1, tiled=True)[0]]
    pallas_call x0 -> x1, Pallas kernels: none -> 94.4 us  [per_device(): pl.pallas_call(kernel, out_shape=(jax.ShapeDtypeStruct((1, TOK, D), bf16)...]
    another operation x66 -> x0, other arithmetic: 86.3 us -> none  [the longest x36 83.2 us: inner_step(): jax.scipy.linalg.solve_triangular(system, right_side, lower=True, unit_di...]
    reduce_scatter x1 -> x0, waiting for transfers between devices: 83.6 us -> none  [per_device(): lax.psum_scatter(lax.dot_general(value_grad, weight_full, (((1,), (1,)),...]
    dot_general x106 -> x0, matrix products: 53.4 us -> none  [the longest x24 7.93 us: inner_step(): new_values = solved[:, head_dim:] - jnp.dot(solved[:, :head_dim], carried)]
    mul x30 -> x0, local copies, waits for them, and re-layouts: 18.4 us -> none  [the longest x16 10.1 us: inner_step(): jnp.exp(cumulative[-1]) * carried]
    ppermute x3 -> x0, waiting for transfers between devices: 9.94 us -> none  [passed_along(): return lax.ppermute(shard, axis, pairs)]
    another operation x12 -> x0, matrix products: 9.86 us -> none  [inner_step(): jax.scipy.linalg.solve_triangular(system, right_side, lower=True, unit_di...]
  transfers between devices with their start and end apart: 7 -> 0, of which waited for: 7 -> 0; matrix products, arithmetic and copies ran while one was open for 2% -> 0% of each run, Pallas kernels for 0% -> 0%
where the time goes in v1:
time: 101 us; the launch traced here: 99.6 us
  Pallas kernels  94.4 us (93%)
  local copies, waits for them, and re-layouts  4.55 us (5%)
    pallas_call x1, Pallas kernels, per_device(): pl.pallas_call(kernel, out_shape=(jax.ShapeDtypeStruct((1, TOK, D), bf16)...  94.4 us
    unnamed x13, local copies, waits for them, and re-layouts  4.55 us

profile of v1, /device:TPU:1, one launch (start us, length us, event | category | flops | bytes accessed | tf_op | source)
XLA Modules:
  0.0 99.6 jit_solution(4236292217919327794)
XLA Ops:
  0.6 94.4 %shard_map.119 = (bf16[1,16,8192]{2,1,0:T(8,128)(2,1)}, bf16[1,256,256]{2,1,0:T(8,128)(2,1)}, bf16[1,256,256]{2,1,0:T(8,128)(2,1)}, f32[2,1,2,256]{3,2,1,0:T(2,128)}, f32[2,2]{1,0:T(2,128)}) custom-call(bf16[16,8192]{1,0:T(8,128)(2,1)} %bitcast.4, bf16[256,256]{1,0:T(8,128)(2,1)} %w_ref.1, bf16[256,256]{1,0:T(8,128)(2,1)} %bitcast.5, ...), custom_call_target="tpu_custom_call" | custom-call | tf_op jit(solution)/shard_map/pallas_call | solution.py:431
  95.0 0.0 copy-start.1
  95.0 1.7 %copy.18 = bf16[1,16,8192]{2,1,0:T(8,128)(2,1)} copy(bf16[1,16,8192]{2,1,0:T(8,128)(2,1)} %get-tuple-element.10) | data formatting | bytes 524288
  96.7 0.0 copy-done.1
  96.7 0.0 copy-start
  96.7 0.7 copy.19
  97.4 0.3 copy-done
  97.7 0.0 copy-start.2
  97.7 0.7 copy.20
  98.3 0.0 copy-done.2
  98.4 0.0 copy-start.3
  98.4 0.6 copy.21
  99.0 0.1 copy-done.3
  99.0 0.6 copy.22
Async XLA Ops:
  95.0 1.7 %copy-start.1 = (bf16[1,256,256]{2,1,0:T(8,128)(2,1)S(1)}, bf16[1,256,256]{2,1,0:T(8,128)(2,1)}, u32[]{:S(2)}) copy-start(bf16[1,256,256]{2,1,0:T(8,128)(2,1)} %get-tuple-element.11) | copy-start | bytes 393220
  96.7 1.0 copy-start
  97.7 0.7 copy-start.2
  98.4 0.7 copy-start.3

commit v2 on v1

--- a/solution.py
+++ b/solution.py
@@ -47,10 +47,10 @@
 def kernel(
     x_ref, w_ref, q_ref, k_ref, do_ref, gl_ref, par_ref, st_ref,
     ig_ref, qg_ref, kg_ref, gg_ref, dg_ref,
-    xs, xg, xl, wg, pcs, pcr, cbs, cbr, dvs, dvg, vp, vr, gl_s, gs, gx, gys, gyr, dct, dzt,
+    xs, xg, xl, wg, pcs, pcr, cbs, cbr, dvg, vp, vss, vrr, gl_s, gs, gx, gys, gyr, tiles,
     qn, kn, dec, a_s, p_s, t_s, ef_s, dr_s, s_in,
     xa_s, xa_r, xx_s, xx_r, wp_s, wp_r, wz_s, wz_r, wd_s, wd_r, pc_s, pc_r, cb_s, cb_r,
-    dv_s, dv_r, vp_s, vp_r, gx_s, gx_r, gy_s, gy_r, dc_s, dc_r, dz_s, dz_r,
+    dv_s, dv_r, vp_s, vp_r, gx_s, gx_r, gy_s, gy_r, dz_s, dz_r,
 ):
     z = lax.axis_index("dp")
     ctx = lax.axis_index("ctx")
@@ -84,7 +84,14 @@
     peers = [at(z, y_at(o), c, x) for o in range(1, YN)]
     peers += [at(z, y_at(o), 1 - c, x) for o in range(YN)]
     peers += [at(z, yy, c, x_at(o)) for o in range(1, XN)]
-    peers += [at(z_at(o), yy, c, x) for o in range(1, ZN)]
+    family = [
+        (at(z_at(o), yy + dy * (1 - 2 * ylo), c + dc * (1 - 2 * c), x), o, dy, dc)
+        for o in range(ZN)
+        for dy in range(2)
+        for dc in range(2)
+        if o + dy + dc > 0
+    ]
+    peers += [device for device, o, dy, dc in family if o > 0]
     for peer in peers:
         pl.semaphore_signal(barrier, inc=1, device_id=peer, device_id_type=MESH)
 
@@ -94,54 +101,6 @@
                 :, z_ * KB + y_ * 128 : z_ * KB + (y_ + 1) * 128
             ]
     xg[x, yy] = xs[yy]
-    pl.semaphore_wait(barrier, len(peers))
-
-    to_core = lax.rem(lax.div(yhi, 2) + 1 + lax.div(ctx, 2) + lax.rem(ctx, 2), 2)
-    own_half = lax.rem(c + 1 + lax.div(yhi, 2) + lax.rem(yhi, 2), 2)
-    w_pre = [
-        send(
-            w_ref.at[pl.ds(h * 128, 128), :],
-            wg.at[lax.div(yhi, 2), z, lax.rem(yhi, 2)],
-            wp_s.at[h],
-            wp_r.at[lax.rem(yhi, 2)],
-            at(z, ctx * 2 + h, to_core, x),
-        )
-        for h in range(2)
-    ]
-    w_pre_in = [
-        send(w_ref.at[pl.ds(0, 128), :], wg.at[own_half, z, h], wp_s.at[h], wp_r.at[h], at(z, yy, 1 - c, x))
-        for h in range(2)
-    ]
-    for copy in w_pre:
-        copy.start()
-    x_all = [
-        send(xs.at[y_at(o)], xg.at[x, yy], xa_s.at[o], xa_r.at[o], at(z, y_at(o), c, x))
-        for o in range(1, YN)
-    ]
-    for copy in x_all:
-        copy.start()
-
-    def w_round():
-        for copy in w_pre_in:
-            copy.wait_recv()
-        for copy in w_sends:
-            copy.start()
-
-    w_sends = [
-        send(wg.at[own_half, z], wg.at[own_half, z], wz_s.at[o], wz_r.at[o], at(z_at(o), yy, c, x))
-        for o in range(1, ZN)
-    ]
-    x_sends = [
-        send(xg.at[x], xg.at[x], xx_s.at[o], xx_r.at[o], at(z, yy, c, x_at(o)))
-        for o in range(1, XN)
-    ]
-
-    def x_round():
-        for copy in x_all:
-            copy.wait_recv()
-        for copy in x_sends:
-            copy.start()
-
     ii = lax.broadcasted_iota(jnp.int32, (N, N), 0)
     jj = lax.broadcasted_iota(jnp.int32, (N, N), 1)
     low = ii >= jj
@@ -178,8 +137,6 @@
         a_s[h] = jnp.where(strict, be_col[h] * dec[h] * mm(kn[h], kn[h], 1, 1), 0.0)
         p_s[h] = dec[h] * mm(qn[h], kn[h], 1, 1)
         t_s[h] = jnp.where(ii == jj, 1.0, jnp.where(apart == 1, -a_s[h], 0.0))
-    w_round()
-
     size = 2
     while size < N:
         for h in range(HEADS):
@@ -187,8 +144,6 @@
             t_b = t_s[h].astype(bf16)
             t_s[h] = t_s[h] - mm(mm(t_b, level), t_b)
         size *= 2
-    x_round()
-
     for h in range(HEADS):
         do_h = head(do_ref, h)
         start = mm(p_s[h], do_h, 0, 0)
@@ -200,8 +155,28 @@
         carry = jnp.where(i2 == j2, gam_n[h], 0.0) - ke[:, HD:]
         pcs[h] = jnp.concatenate([carry, const], axis=1).astype(bf16)
 
+    pl.semaphore_wait(barrier, len(peers))
+
     to_partner = send(pcs, pcr, pc_s, pc_r, at(z, yy, 1 - c, x))
     to_partner.start()
+    to_core = lax.rem(lax.div(yhi, 2) + 1 + lax.div(ctx, 2) + lax.rem(ctx, 2), 2)
+    own_half = lax.rem(c + 1 + lax.div(yhi, 2) + lax.rem(yhi, 2), 2)
+    w_pre = [
+        send(
+            w_ref.at[pl.ds(h * 128, 128), :],
+            wg.at[lax.div(yhi, 2), z, lax.rem(yhi, 2)],
+            wp_s.at[h],
+            wp_r.at[lax.rem(yhi, 2)],
+            at(z, ctx * 2 + h, to_core, x),
+        )
+        for h in range(2)
+    ]
+    w_pre_in = [
+        send(w_ref.at[pl.ds(0, 128), :], wg.at[own_half, z, h], wp_s.at[h], wp_r.at[h], at(z, yy, 1 - c, x))
+        for h in range(2)
+    ]
+    for copy in w_pre:
+        copy.start()
     to_partner.wait_recv()
     other_y = yy + 1 - 2 * ylo
     even = c == 0
@@ -212,6 +187,75 @@
         cbs[h] = (mm(first[:, :HD], last[:, HD:]) + first[:, HD:].astype(f32)).astype(bf16)
     to_other = send(cbs, cbr, cb_s, cb_r, at(z, other_y, c, x))
     to_other.start()
+    x_all = [
+        send(xs.at[y_at(o)], xg.at[x, yy], xa_s.at[o], xa_r.at[o], at(z, y_at(o), c, x))
+        for o in range(1, YN)
+    ]
+    for copy in x_all:
+        copy.start()
+
+    def z_hop(way, k, half):
+        slot = wg.at[own_half, z_at(ZN - k if way == 0 else k), half]
+        return send(
+            slot, slot, wz_s.at[way, k, half], wz_r.at[way, k, half],
+            at(z_at(1 if way == 0 else ZN - 1), yy, c, x),
+        )
+
+    def z_arrival(way, k, half):
+        slot = wg.at[own_half, z_at(ZN - 1 - k if way == 0 else k + 1), half]
+        return send(
+            slot, slot, wz_s.at[way, k, half], wz_r.at[way, k, half],
+            at(z_at(1 if way == 0 else ZN - 1), yy, c, x),
+        )
+
+    def y_hop(way, k, half):
+        slot = dvg.at[y_at(YN - k if way == 0 else k), pl.ds(half * 128, 128), :]
+        return send(
+            slot, slot, dv_s.at[way, k, half], dv_r.at[way, k, half],
+            at(z, y_at(1 if way == 0 else YN - 1), c, x),
+        )
+
+    def y_arrival(way, k, half):
+        slot = dvg.at[y_at(YN - 1 - k if way == 0 else k + 1), pl.ds(half * 128, 128), :]
+        return send(
+            slot, slot, dv_s.at[way, k, half], dv_r.at[way, k, half],
+            at(z, y_at(1 if way == 0 else YN - 1), c, x),
+        )
+
+    ring_sends = []
+
+    def launch(copy):
+        copy.start()
+        ring_sends.append(copy)
+
+    def relay(hop, arrival, k):
+        for turn in range(2):
+            for way in range(2):
+                half = turn if way == 0 else 1 - turn
+                if k == 3 and half != way:
+                    continue
+                arrival(way, k, half).wait_recv()
+                if k < 2 or (k == 2 and half == way):
+                    launch(hop(way, k + 1, half))
+
+    def share(o):
+        slot = wg.at[own_half, z_at(o)]
+        return send(slot, slot, wd_s.at[o], wd_r.at[o], at(z, yy, 1 - c, x))
+
+    def x_forward(o):
+        x_all[o - 1].wait_recv()
+        slot = xg.at[x, y_at(YN - o)]
+        for p in range(1, XN):
+            launch(send(slot, slot, xx_s.at[p, o], xx_r.at[p, o], at(z, yy, c, x_at(p))))
+
+    for p in range(1, XN):
+        slot = xg.at[x, yy]
+        launch(send(slot, slot, xx_s.at[p, 0], xx_r.at[p, 0], at(z, yy, c, x_at(p))))
+    for half in range(2):
+        w_pre_in[half].wait_recv()
+        for way in range(2):
+            launch(z_hop(way, 0, half))
+    launch(share(0))
     to_other.wait_recv()
     for h in range(HEADS):
         inward = jnp.where(ylo == 0, cbr[h], jnp.zeros((HD, HD), bf16))
@@ -220,49 +264,79 @@
         s_in[h] = jnp.where(even, through, inward.astype(f32))
         dr = ef_s[h][:, :HD] + mm(ef_s[h][:, HD:], s_in[h])
         dr_s[h] = dr
-        dvs[:, h * HD : (h + 1) * HD] = (be_col[h] * dr).astype(bf16)
-    dv_sends = [
-        send(dvs, dvg.at[yy], dv_s.at[o], dv_r.at[o], at(z, y_at(o), c, x)) for o in range(1, YN)
-    ]
-    for copy in dv_sends:
-        copy.start()
-    dvg[yy] = dvs[...]
-
-    for copy in w_sends:
-        copy.wait_recv()
-    w_share = send(wg.at[own_half], wg.at[own_half], wd_s, wd_r, at(z, yy, 1 - c, x))
-    w_share.start()
-    for copy in x_sends:
-        copy.wait_recv()
+        dvg[yy, :, h * HD : (h + 1) * HD] = (be_col[h] * dr).astype(bf16)
+    for half in range(2):
+        for way in range(2):
+            launch(y_hop(way, 0, half if way == 0 else 1 - half))
+    for o in (1, 7, 2, 6):
+        x_forward(o)
+    relay(z_hop, z_arrival, 0)
+    launch(share(1))
+    launch(share(7))
+    for o in (3, 5, 4):
+        x_forward(o)
+    relay(y_hop, y_arrival, 0)
+    relay(z_hop, z_arrival, 1)
+    launch(share(2))
+    launch(share(6))
+    relay(y_hop, y_arrival, 1)
+    relay(z_hop, z_arrival, 2)
+    launch(share(3))
+    launch(share(5))
+    relay(y_hop, y_arrival, 2)
+    relay(z_hop, z_arrival, 3)
+    launch(share(4))
+    for p in range(1, XN):
+        for o in range(YN):
+            slot = xg.at[x_at(XN - p), y_at(YN - o)]
+            send(slot, slot, xx_s.at[p, o], xx_r.at[p, o], at(z, yy, c, x_at(p))).wait_recv()
     for x_ in range(XN):
         for y_ in range(YN):
             row = (y_ % 2) * N + ((y_ // 2) * XN + x_) * TOK
             xl[row : row + TOK, :] = xg[x_, y_]
-    w_share.wait_recv()
+    for o in range(ZN):
+        slot = wg.at[1 - own_half, z_at(o)]
+        send(slot, slot, wd_s.at[o], wd_r.at[o], at(z, yy, 1 - c, x)).wait_recv()
 
     def weight(y_hi):
         return wg[lax.div(y_hi, 2), :, lax.rem(y_hi, 2)].reshape(KB, N)
 
     def v_piece(o, _):
-        d = lax.rem(yy + o, YN)
+        d = lax.rem(yy + 4 + (1 - 2 * lax.rem(o, 2)) * lax.div(o + 1, 2), YN)
         rows_in = xl[pl.ds(pl.multiple_of(lax.rem(d, 2) * N, N), N), :]
         vp[d] = mm(rows_in, weight(lax.div(d, 2))).astype(bf16)
         return 0
 
-    def v_send(o):
-        return send(vp.at[y_at(o)], vr.at[yy], vp_s.at[o], vp_r.at[o], at(z, y_at(o), c, x))
-
-    def v_step(o, _):
-        v_piece(o, 0)
-        v_send(o).start()
-        return 0
-
-    lax.fori_loop(1, YN, v_step, 0)
-    v_piece(0, 0)
-    vr[yy] = vp[yy]
-
-    for copy in dv_sends:
-        copy.wait_recv()
+    def v_hop(way, e):
+        if e < 2:
+            half = e if way == 0 else 1 - e
+            d = y_at(4 - e if way == 0 else 4 + e)
+            source = vp.at[d, pl.ds(half * 128, 128), :]
+        else:
+            source = vss.at[way, e - 2]
+        return send(
+            source, vrr.at[way, e], vp_s.at[way, e], vp_r.at[way, e],
+            at(z, y_at(1 if way == 0 else YN - 1), c, x),
+        )
+
+    def v_relay(e):
+        for way in range(2):
+            v_hop(way, e).wait_recv()
+            if e < 5:
+                left = 3 - (e + 1) // 2
+                half = e % 2 if way == 0 else 1 - e % 2
+                d = y_at(left if way == 0 else YN - left)
+                own = vp[d, half * 128 : half * 128 + 128, :]
+                vss[way, e] = (vrr[way, e].astype(f32) + own.astype(f32)).astype(bf16)
+                launch(v_hop(way, e + 2))
+
+    lax.fori_loop(0, 3, v_piece, 0)
+    for e in range(2):
+        for way in range(2):
+            launch(v_hop(way, e))
+    lax.fori_loop(3, YN, v_piece, 0)
+
+    relay(y_hop, y_arrival, 3)
 
     def g_piece(o):
         x_to = x_at(o)
@@ -280,16 +354,21 @@
     def g_send(o):
         return send(gs.at[x_at(o)], gx.at[x], gx_s.at[o], gx_r.at[o], at(z, yy, c, x_at(o)))
 
-    def g_step(o, _):
-        g_piece(o)
-        g_send(o).start()
-        return 0
-
-    lax.fori_loop(1, XN, g_step, 0)
+    g_piece(2)
+    launch(g_send(2))
+    v_relay(0)
+    v_relay(1)
+    g_piece(1)
+    launch(g_send(1))
+    v_relay(2)
+    g_piece(3)
+    launch(g_send(3))
+    v_relay(3)
     g_piece(0)
+    gx[x] = gs[x]
+    v_relay(4)
     for o in range(1, XN):
         g_send(o).wait_recv()
-    gx[x] = gs[x]
     gys[...] = (
         (gx[0].astype(f32) + gx[1].astype(f32)) + (gx[2].astype(f32) + gx[3].astype(f32))
     ).astype(bf16)
@@ -304,12 +383,13 @@
         copy.start()
     gyr[yy] = gys[pl.ds(pl.multiple_of(yy * TOK, TOK), TOK), :]
 
-    for o in range(1, YN):
-        v_send(o).wait_recv()
-    values = vr[0].astype(f32)
-    for y_ in range(1, YN):
-        values = values + vr[y_].astype(f32)
-    dvs2 = values.astype(bf16)
+    v_relay(5)
+    v_relay(6)
+    halves = []
+    for half in range(2):
+        ways = vrr[0, 6 - half].astype(f32) + vrr[1, 5 + half].astype(f32)
+        halves.append(vp[yy, half * 128 : half * 128 + 128, :].astype(f32) + ways)
+    dvs2 = jnp.concatenate(halves, axis=0).astype(bf16)
     lane = lax.broadcasted_iota(jnp.int32, (N, HD), 1)
     picked = jnp.zeros((N, HD), f32)
     dg_rows = []
@@ -372,24 +452,15 @@
     bias_sum = jnp.sum(d_ga, axis=1, keepdims=True)
     lane2 = lax.broadcasted_iota(jnp.int32, (HEADS, 128), 1)
     mine = jnp.where(lane2 == 0, scale_sum, jnp.where(lane2 == 1, bias_sum, 0.0))
-    dct[ctx] = jnp.concatenate([mine, jnp.zeros((6, 128), f32)], axis=0)
-    dc_sends = []
-    for o, (dy, dc) in enumerate(((0, 1), (1, 0), (1, 1))):
-        y_to = yy + dy * (1 - 2 * ylo)
-        c_to = c + dc * (1 - 2 * c)
-        dc_sends.append(send(dct.at[ctx], dct.at[ctx], dc_s.at[o], dc_r.at[o], at(z, y_to, c_to, x)))
-    for copy in dc_sends:
+    own_tile = z * 4 + ctx
+    tiles[own_tile] = jnp.concatenate([mine, jnp.zeros((6, 128), f32)], axis=0)
+    tile_sends = []
+    for device, o, dy, dc in family:
+        number = o * 4 + dy * 2 + dc
+        slot = tiles.at[own_tile]
+        copy = send(slot, slot, dz_s.at[number], dz_r.at[number], device)
         copy.start()
-    for copy in dc_sends:
-        copy.wait_recv()
-    dzt[z] = (dct[0] + dct[1]) + (dct[2] + dct[3])
-    dz_sends = [
-        send(dzt.at[z], dzt.at[z], dz_s.at[o], dz_r.at[o], at(z_at(o), yy, c, x))
-        for o in range(1, ZN)
-    ]
-    for copy in dz_sends:
-        copy.start()
-
+        tile_sends.append(copy)
     for copy in gy_sends:
         copy.wait_recv()
     for y_ in range(YN):
@@ -397,26 +468,18 @@
             ig_ref[0, :, z_ * KB + y_ * 128 : z_ * KB + (y_ + 1) * 128] = gyr[
                 y_, :, z_ * 128 : (z_ + 1) * 128
             ]
-    for copy in dz_sends:
+    for copy in tile_sends:
         copy.wait_recv()
-    grand = dzt[0]
-    for z_ in range(1, ZN):
-        grand = grand + dzt[z_]
+    grand = tiles[0]
+    for tile in range(1, 4 * ZN):
+        grand = grand + tiles[tile]
     dg_ref[...] = pair(
         (2, 2), 0,
         pair((2, 2), 1, grand[0:1, 0:1], grand[1:2, 0:1]),
         pair((2, 2), 1, grand[0:1, 1:2], grand[1:2, 1:2]),
     )
 
-    for copy in w_pre + x_all + w_sends + x_sends:
-        copy.wait_send()
-    for copy in [to_partner, to_other, w_share] + dv_sends:
-        copy.wait_send()
-    for o in range(1, YN):
-        v_send(o).wait_send()
-    for o in range(1, XN):
-        g_send(o).wait_send()
-    for copy in gy_sends + dc_sends + dz_sends:
+    for copy in w_pre + x_all + [to_partner, to_other] + ring_sends + gy_sends + tile_sends:
         copy.wait_send()
 
 
@@ -426,8 +489,7 @@
     vmem = pl.BlockSpec(memory_space=pltpu.VMEM)
     dma = pltpu.SemaphoreType.DMA
     V = pltpu.VMEM
-    counts = (8, 8, 4, 4, 2, 2, 8, 8, None, None, None, None, None, None)
-    counts += (8, 8, 8, 8, 4, 4, 8, 8, 3, 3, 8, 8)
+    counts = [(8,), (4, 8), (2,), (2, 4, 2), (8,), (), (), (2, 4, 2), (2, 7), (4,), (8,), (32,)]
     return pl.pallas_call(
         kernel,
         out_shape=(
@@ -448,17 +510,16 @@
             V((HEADS, HD, 2 * HD), bf16),
             V((HEADS, HD, HD), bf16),
             V((HEADS, HD, HD), bf16),
-            V((N, N), bf16),
             V((YN, N, N), bf16),
             V((YN, N, N), bf16),
-            V((YN, N, N), bf16),
+            V((2, 5, 128, N), bf16),
+            V((2, 7, 128, N), bf16),
             V((YN * TOK, KB), bf16),
             V((XN, YN * TOK, KB), bf16),
             V((XN, YN * TOK, KB), bf16),
             V((YN * TOK, KB), bf16),
             V((YN, TOK, KB), bf16),
-            V((4, 8, 128), f32),
-            V((ZN, 8, 128), f32),
+            V((4 * ZN, 8, 128), f32),
             V((HEADS, N, HD), f32),
             V((HEADS, N, HD), f32),
             V((HEADS, N, N), f32),
@@ -469,7 +530,7 @@
             V((HEADS, N, HD), f32),
             V((HEADS, HD, HD), f32),
         ]
-        + [dma(()) if n is None else dma((n,)) for n in counts],
+        + [dma(n) for n in counts for _ in range(2)],
         compiler_params=pltpu.CompilerParams(
             collective_id=0, has_side_effects=True, vmem_limit_bytes=56 * 2**20
         ),

time: 101 us -> 78.7 us (0.78); the launches traced: 99.6 us -> 78.5 us
  Pallas kernels: 94.4 us -> 73.3 us
    pallas_call x1, Pallas kernels: 94.4 us -> 73.3 us  [per_device(): pl.pallas_call(kernel, out_shape=(jax.ShapeDtypeStruct((1, TOK, D), bf16)...]
where the time goes in v2:
time: 78.7 us; the launch traced here: 78.5 us
  Pallas kernels  73.3 us (93%)
  local copies, waits for them, and re-layouts  4.55 us (6%)
    pallas_call x1, Pallas kernels, per_device(): pl.pallas_call(kernel, out_shape=(jax.ShapeDtypeStruct((1, TOK, D), bf16)...  73.3 us
    unnamed x13, local copies, waits for them, and re-layouts  4.55 us

profile of v2, /device:TPU:1, one launch (start us, length us, event | category | flops | bytes accessed | tf_op | source)
XLA Modules:
  0.0 78.5 jit_solution(16565846961020516154)
XLA Ops:
  0.6 73.3 %shard_map.119 = (bf16[1,16,8192]{2,1,0:T(8,128)(2,1)}, bf16[1,256,256]{2,1,0:T(8,128)(2,1)}, bf16[1,256,256]{2,1,0:T(8,128)(2,1)}, f32[2,1,2,256]{3,2,1,0:T(2,128)}, f32[2,2]{1,0:T(2,128)}) custom-call(bf16[16,8192]{1,0:T(8,128)(2,1)} %bitcast.4, bf16[256,256]{1,0:T(8,128)(2,1)} %w_ref.1, bf16[256,256]{1,0:T(8,128)(2,1)} %bitcast.5, ...), custom_call_target="tpu_custom_call" | custom-call | tf_op jit(solution)/shard_map/pallas_call | solution.py:493
  73.9 0.0 copy-start.1
  74.0 1.7 %copy.18 = bf16[1,16,8192]{2,1,0:T(8,128)(2,1)} copy(bf16[1,16,8192]{2,1,0:T(8,128)(2,1)} %get-tuple-element.10) | data formatting | bytes 524288
  75.7 0.0 copy-done.1
  75.7 0.0 copy-start
  75.7 0.7 copy.19
  76.3 0.3 copy-done
  76.6 0.0 copy-start.2
  76.6 0.7 copy.20
  77.3 0.0 copy-done.2
  77.3 0.0 copy-start.3
  77.3 0.6 copy.21
  77.9 0.1 copy-done.3
  78.0 0.6 copy.22
Async XLA Ops:
  73.9 1.7 %copy-start.1 = (bf16[1,256,256]{2,1,0:T(8,128)(2,1)S(1)}, bf16[1,256,256]{2,1,0:T(8,128)(2,1)}, u32[]{:S(2)}) copy-start(bf16[1,256,256]{2,1,0:T(8,128)(2,1)} %get-tuple-element.11) | copy-start | bytes 393220
  75.7 1.0 %copy-start = (bf16[1,256,256]{2,1,0:T(8,128)(2,1)S(1)}, bf16[1,256,256]{2,1,0:T(8,128)(2,1)}, u32[]{:S(2)}) copy-start(bf16[1,256,256]{2,1,0:T(8,128)(2,1)} %get-tuple-element.12) | copy-start | bytes 393220
  76.6 0.7 copy-start.2
  77.3 0.7 copy-start.3
